TPU v7x, 32 devices: a whole 2x2x4 slice. The times are simulated.
32 devices in a mesh: curve: 8 (over z, x), head: 4 (over y, core).
Axes of the slice: x: 2, y: 2, z: 4, core: 2. Of those that a mesh axis runs over, the one named last changes fastest.
Arguments:
- points: bfloat16 [16384, 1024], P(('curve', 'head')), may hold values from -6 to 6
- order: int32 [32, 512], P(('curve', 'head')), may hold values from 0 to 511, each once within a row
- scan_ids: int32 [16384], P(('curve', 'head')), may hold values from 0 to 3
- ln_gain: float32 [2, 1024], replicated, may hold values from 0.25 to 1.75
- w_qkv: bfloat16 [2, 1024, 3072], P(None, None, 'head'), may hold values from -7 to 7, as said below
- w_out: bfloat16 [2, 1024, 1024], P(None, 'head'), may hold values from -0.1875 to 0.1875
Outputs:
- refined: bfloat16 [16384, 1024], P(('curve', 'head'))
Inputs may be any that keep to these rules, and one draw needn't show every extreme that they name: `order`: row b is a permutation of the 512 rows of block b. `w_qkv`: columns ordered by head, then query, key, value, then entry.
All inputs are finite; a program needn't handle non-finite values.
Results may differ from a plain program's by a relative error of at most 0.01.
Values may be sent and summed in bfloat16 or wider, within the bound.
A program may use at most 64 MiB of HBM per device.

v0:
```python
import jax
import jax.numpy as jnp
from jax import lax
from jax.sharding import PartitionSpec as P

HEAD_DIM = 64
PATCH = 1024


EPSILON = 1e-05


def extended(array, sides, width):
    for axis, dim in sides:
        peers, length = (lax.axis_size(axis), array.shape[dim])
        up = [(i, (i + 1) % peers) for i in range(peers)]
        down = [(j, i) for i, j in up]
        last = lax.slice_in_dim(array, length - width, length, axis=dim)
        first = lax.slice_in_dim(array, 0, width, axis=dim)
        before = lax.ppermute(last, axis, up)
        after = lax.ppermute(first, axis, down)
        array = jnp.concatenate([before, array, after], axis=dim)
    return array


def layer_norm(rows, gain):
    values = rows.astype(jnp.float32)
    center = values - jnp.mean(values, axis=-1, keepdims=True)
    spread = jnp.mean(center * center, axis=-1, keepdims=True)
    return (center * lax.rsqrt(spread + EPSILON) * gain).astype(jnp.bfloat16)


def plain_window(first_row):
    return first_row // PATCH * PATCH


def centred_window(first_row):
    return (first_row + PATCH // 2) // PATCH * PATCH


def attend(queries, keys, values, query_tags, key_tags, window_of):
    block_rows = PATCH // 2
    blocks_count = queries.shape[0] // block_rows

    def one_block(block_index):
        first_row = block_index * block_rows
        query_block = lax.dynamic_slice_in_dim(queries, first_row, block_rows, 0)
        tags_block = lax.dynamic_slice_in_dim(query_tags, first_row, block_rows, 0)
        first_key = window_of(first_row)
        key_block = lax.dynamic_slice_in_dim(keys, first_key, PATCH, 0)
        value_block = lax.dynamic_slice_in_dim(values, first_key, PATCH, 0)
        key_block_tags = lax.dynamic_slice_in_dim(key_tags, first_key, PATCH, 0)
        scores = jnp.einsum(
            "qhd,khd->hqk", query_block, key_block, preferred_element_type=jnp.float32
        ) * HEAD_DIM ** (-0.5)
        allowed = tags_block[:, None] == key_block_tags[None, :]
        scores = jnp.where(allowed[None], scores, -jnp.inf)
        row_max = jnp.max(scores, axis=-1, keepdims=True)
        expo = jnp.exp(scores - row_max)
        probs = (expo / jnp.sum(expo, axis=-1, keepdims=True)).astype(jnp.bfloat16)
        result = jnp.einsum("hqk,khd->qhd", probs, value_block, preferred_element_type=jnp.float32)
        return result.astype(jnp.bfloat16)

    outputs = lax.map(one_block, jnp.arange(blocks_count))
    return outputs.reshape(queries.shape[0], -1)


def on_device(points, order, scan_ids, ln_gain, w_qkv, w_out):
    stream = points[order[0]]
    range_ids = lax.all_gather(scan_ids, "head", axis=0, tiled=True)
    span_rows = range_ids.shape[0]
    heads_local = w_qkv.shape[2] // (3 * HEAD_DIM)
    half_patch = PATCH // 2
    for layer_index in range(2):
        normed = layer_norm(stream, ln_gain[layer_index])
        weights_here = w_qkv[layer_index]
        qkv_span = jnp.dot(
            lax.all_gather(normed, "head", axis=0, tiled=True),
            weights_here,
            preferred_element_type=jnp.float32,
        ).astype(jnp.bfloat16)
        pieces = qkv_span.reshape(span_rows, heads_local, 3, HEAD_DIM)
        if layer_index == 0:
            attended = attend(
                pieces[:, :, 0],
                pieces[:, :, 1],
                pieces[:, :, 2],
                range_ids,
                range_ids,
                plain_window,
            )
        else:
            tags_float = range_ids.astype(jnp.bfloat16)
            kv_flat = pieces[:, :, 1:].reshape(span_rows, heads_local * 2 * HEAD_DIM)
            wide_kv, wide_tags = (
                extended(kv_flat, (("curve", 0),), half_patch),
                extended(tags_float, (("curve", 0),), half_patch),
            )
            wide_pieces = wide_kv.reshape(-1, heads_local, 2, HEAD_DIM)
            attended = attend(
                pieces[:, :, 0],
                wide_pieces[:, :, 0],
                wide_pieces[:, :, 1],
                range_ids,
                wide_tags.astype(jnp.int32),
                centred_window,
            )
        heads_rows = lax.all_to_all(attended, "head", split_axis=0, concat_axis=1, tiled=True)
        update = jnp.dot(
            heads_rows,
            lax.all_gather(w_out[layer_index], "head", axis=0, tiled=True),
            preferred_element_type=jnp.float32,
        )
        stream = (stream.astype(jnp.float32) + update).astype(jnp.bfloat16)
    return stream


def solution(mesh):
    in_specs = (
        P(("curve", "head"), None),
        P(("curve", "head"), None),
        P(("curve", "head")),
        P(),
        P(None, None, "head"),
        P(None, "head", None),
    )
    out_specs = P(("curve", "head"), None)
    return jax.shard_map(
        on_device, mesh=mesh, in_specs=in_specs, out_specs=out_specs, check_vma=False
    )
```

profile of v0, /device:TPU:0, one launch (start us, length us, event | category | flops | bytes accessed | tf_op | source)
XLA Modules:
  0.0 295.6 jit_solution(13849537120225569016)
XLA Ops:
  6.5 0.8 compare_select_fusion
  7.3 0.5 copy-done
  7.8 2.0 gather_fusion
  10.1 0.4 fusion.67
  10.5 1.3 fusion.69
  12.0 1.1 fusion.103
  13.1 6.2 %all-gather.2 = s32[4,1,512]{2,1,0:T(1,128)S(1)} all-gather(s32[1,1,512]{2,1,0:T(1,128)S(1)} %bitcast.103), channel_id=1, replica_groups=mesh['curve'=8,'head'=4] {'head'}, dimensions={0}, use_global_device_ids=true | all-gather | bytes 10240 | tf_op jit(solution)/shard_map/all_gather | solution.py:70
  19.3 29.9 %all-gather.8.cloned.1.call-done = bf16[2048,1024]{1,0:T(8,128)(2,1)} async-done(((bf16[512,1024]{1,0:T(8,128)(2,1)}), bf16[2048,1024]{1,0:T(8,128)(2,1)}) %all-gather.8.cloned.1.call-update) | async-done | bytes 4194320 | tf_op jit(solution)/shard_map/all_gather | solution.py:78
  49.2 6.1 %convolution_convert_fusion.1 = bf16[2048,768]{0,1:T(8,128)(2,1)S(1)} fusion(bf16[2048,1024]{1,0:T(8,128)(2,1)} %all-gather.8.cloned.1.call-done, bf16[2,1024,768]{2,1,0:T(8,128)(2,1)} %param.14), kind=kOutput, calls=%fused_computation.52 | convolution fusion | flops 3222798336 | bytes 8912896 | tf_op jit(solution)/shard_map/dot_general | solution.py:77
  55.4 1.7 slice_bitcast_fusion.3
  57.0 1.1 broadcast.125.clone
  58.1 58.1 %while.24 = (s32[]{:T(128)}, bf16[4,512,4,64]{1,3,2,0:T(8,128)(2,1)}, s32[4]{0:T(128)S(1)}, bf16[2048,4,64]{0,2,1:T(8,128)(2,1)}, s32[2048]{0:T(1024)S(1)}, /*in...) while((s32[]{:T(128)}, ...), condition=%wide.region_5.6_spmd, body=%wide.region_2.5_spmd.sunk | while | flops 550110208 | bytes 19434388 | solution.py:64
  58.1 0.6 dynamic_slice.136
  59.5 0.4 broadcast_compare_fusion.4
  59.9 7.0 %fusion.123 = (f32[4,512]{1,0:T(4,128)S(1)}, f32[4,512,1024]{2,1,0:T(8,128)}) fusion(pred[512,1024]{1,0:T(8,128)(4,1)S(1)} %broadcast_compare_fusion.4, bf16[2048,4,64]{0,2,1:T(8,128)(2,1)S(1)} %get-tuple-element.384, s32[]{:T(128)S(6)} %select_n.99, bf16[2048,4,64]{0,2,1:T(8,128)(2,1)} %get-tuple-element.383, s32[]{:T(128)S(6)} %select_n.100), kind=kOutput, calls=%fused_computation.93.clone.1 | convolution fusion | flops 276825088 | bytes 9707528 | tf_op jit(solution)/shard_map/while/body/eval_jaxpr/sub | solution.py:59
  66.9 5.8 %fusion.124 = bf16[4,512,4,64]{1,3,2,0:T(8,128)(2,1)} fusion(bf16[4,512,4,64]{1,3,2,0:T(8,128)(2,1)} %get-tuple-element.364, s32[]{:T(128)} %get-tuple-element.363, f32[4,512,1024]{2,1,0:T(8,128)} %get-tuple-element.336, f32[4,512]{1,0:T(4,128)S(1)} %get-tuple-element.337, bf16[2048,4,64]{0,2,1:T(8,128)(2,1)} %get-tuple-element.381, s32[]{:T(128)S(6)} %select_n.99), kind=kOutput, calls=%fused_computation.12.clone.1 | convolution fusion | flops 272760832 | bytes 9183748 | tf_op jit(solution)/shard_map/while/body/eval_jaxpr/hqk,khd->qhd/dot_general | solution.py:61
  72.7 0.6 dynamic_slice.136
  74.0 0.4 broadcast_compare_fusion.4
  74.4 7.0 %fusion.123 = (f32[4,512]{1,0:T(4,128)S(1)}, f32[4,512,1024]{2,1,0:T(8,128)}) fusion(pred[512,1024]{1,0:T(8,128)(4,1)S(1)} %broadcast_compare_fusion.4, bf16[2048,4,64]{0,2,1:T(8,128)(2,1)S(1)} %get-tuple-element.384, s32[]{:T(128)S(6)} %select_n.99, bf16[2048,4,64]{0,2,1:T(8,128)(2,1)} %get-tuple-element.383, s32[]{:T(128)S(6)} %select_n.100), kind=kOutput, calls=%fused_computation.93.clone.1 | convolution fusion | flops 276825088 | bytes 9707528 | tf_op jit(solution)/shard_map/while/body/eval_jaxpr/sub | solution.py:59
  81.4 5.7 %fusion.124 = bf16[4,512,4,64]{1,3,2,0:T(8,128)(2,1)} fusion(bf16[4,512,4,64]{1,3,2,0:T(8,128)(2,1)} %get-tuple-element.364, s32[]{:T(128)} %get-tuple-element.363, f32[4,512,1024]{2,1,0:T(8,128)} %get-tuple-element.336, f32[4,512]{1,0:T(4,128)S(1)} %get-tuple-element.337, bf16[2048,4,64]{0,2,1:T(8,128)(2,1)} %get-tuple-element.381, s32[]{:T(128)S(6)} %select_n.99), kind=kOutput, calls=%fused_computation.12.clone.1 | convolution fusion | flops 272760832 | bytes 9183748 | tf_op jit(solution)/shard_map/while/body/eval_jaxpr/hqk,khd->qhd/dot_general | solution.py:61
  87.2 0.6 dynamic_slice.136
  88.6 0.4 broadcast_compare_fusion.4
  88.9 7.0 %fusion.123 = (f32[4,512]{1,0:T(4,128)S(1)}, f32[4,512,1024]{2,1,0:T(8,128)}) fusion(pred[512,1024]{1,0:T(8,128)(4,1)S(1)} %broadcast_compare_fusion.4, bf16[2048,4,64]{0,2,1:T(8,128)(2,1)S(1)} %get-tuple-element.384, s32[]{:T(128)S(6)} %select_n.99, bf16[2048,4,64]{0,2,1:T(8,128)(2,1)} %get-tuple-element.383, s32[]{:T(128)S(6)} %select_n.100), kind=kOutput, calls=%fused_computation.93.clone.1 | convolution fusion | flops 276825088 | bytes 9707528 | tf_op jit(solution)/shard_map/while/body/eval_jaxpr/sub | solution.py:59
  95.9 5.7 %fusion.124 = bf16[4,512,4,64]{1,3,2,0:T(8,128)(2,1)} fusion(bf16[4,512,4,64]{1,3,2,0:T(8,128)(2,1)} %get-tuple-element.364, s32[]{:T(128)} %get-tuple-element.363, f32[4,512,1024]{2,1,0:T(8,128)} %get-tuple-element.336, f32[4,512]{1,0:T(4,128)S(1)} %get-tuple-element.337, bf16[2048,4,64]{0,2,1:T(8,128)(2,1)} %get-tuple-element.381, s32[]{:T(128)S(6)} %select_n.99), kind=kOutput, calls=%fused_computation.12.clone.1 | convolution fusion | flops 272760832 | bytes 9183748 | tf_op jit(solution)/shard_map/while/body/eval_jaxpr/hqk,khd->qhd/dot_general | solution.py:61
  101.7 0.6 dynamic_slice.136
  103.1 0.4 broadcast_compare_fusion.4
  103.4 7.0 %fusion.123 = (f32[4,512]{1,0:T(4,128)S(1)}, f32[4,512,1024]{2,1,0:T(8,128)}) fusion(pred[512,1024]{1,0:T(8,128)(4,1)S(1)} %broadcast_compare_fusion.4, bf16[2048,4,64]{0,2,1:T(8,128)(2,1)S(1)} %get-tuple-element.384, s32[]{:T(128)S(6)} %select_n.99, bf16[2048,4,64]{0,2,1:T(8,128)(2,1)} %get-tuple-element.383, s32[]{:T(128)S(6)} %select_n.100), kind=kOutput, calls=%fused_computation.93.clone.1 | convolution fusion | flops 276825088 | bytes 9707528 | tf_op jit(solution)/shard_map/while/body/eval_jaxpr/sub | solution.py:59
  110.5 5.7 %fusion.124 = bf16[4,512,4,64]{1,3,2,0:T(8,128)(2,1)} fusion(bf16[4,512,4,64]{1,3,2,0:T(8,128)(2,1)} %get-tuple-element.364, s32[]{:T(128)} %get-tuple-element.363, f32[4,512,1024]{2,1,0:T(8,128)} %get-tuple-element.336, f32[4,512]{1,0:T(4,128)S(1)} %get-tuple-element.337, bf16[2048,4,64]{0,2,1:T(8,128)(2,1)} %get-tuple-element.381, s32[]{:T(128)S(6)} %select_n.99), kind=kOutput, calls=%fused_computation.12.clone.1 | convolution fusion | flops 272760832 | bytes 9183748 | tf_op jit(solution)/shard_map/while/body/eval_jaxpr/hqk,khd->qhd/dot_general | solution.py:61
  116.2 3.5 %all-to-all-start = ((bf16[4,512,256]{1,2,0:T(8,128)(2,1)}), bf16[4,512,256]{1,2,0:T(8,128)(2,1)S(1)}, u32[]{:S(2)}, u32[]{:S(2)}) async-start(bf16[4,512,256]{1,2,0:T(8,128)(2,1)} %bitcast.16), calls=%async_computation | async-start | bytes 2097152 | tf_op jit(solution)/shard_map/all_to_all | solution.py:108
  120.0 14.1 %all-to-all-done = bf16[4,512,256]{1,2,0:T(8,128)(2,1)S(1)} async-done(((bf16[4,512,256]{1,2,0:T(8,128)(2,1)}), bf16[4,512,256]{1,2,0:T(8,128)(2,1)S(1)}, u32[]{:S(2)}, u32[]{:S(2)}) %all-to-all-start) | async-done | bytes 1048608 | tf_op jit(solution)/shard_map/all_to_all | solution.py:108
  134.1 2.9 convert_reduce_fusion
  137.1 0.4 fusion.64
  137.5 1.4 fusion.66
  139.0 1.5 collective-permute-start.2
  140.5 3.3 %collective-permute-start.3 = (bf16[512]{0:T(512)(128)(2,1)S(1)}, bf16[512]{0:T(512)(128)(2,1)S(1)}, u32[]{:S(2)}, u32[]{:S(2)}) collective-permute-start(bf16[512]{0:T(512)(128)(2,1)S(1)} %get-tuple-element.245), channel_id=1, source_target_pairs={{4,0},{8,4},{12,8},{16,12},{20,16},{24,20},{28,24},{0,28},{5,1},{9... | collective-permute-start | bytes 3080 | tf_op jit(solution)/shard_map/ppermute | solution.py:21
  143.8 29.7 %all-gather.10.cloned.1.call-done = bf16[2048,1024]{1,0:T(8,128)(2,1)} async-done(((bf16[512,1024]{1,0:T(8,128)(2,1)}), bf16[2048,1024]{1,0:T(8,128)(2,1)}) %all-gather.10.cloned.1.call-update) | async-done | bytes 4194320 | tf_op jit(solution)/shard_map/all_gather | solution.py:78
  173.5 6.1 %convolution_convert_fusion = bf16[2048,768]{0,1:T(8,128)(2,1)S(1)} fusion(bf16[2048,1024]{1,0:T(8,128)(2,1)} %all-gather.10.cloned.1.call-done, bf16[2,1024,768]{2,1,0:T(8,128)(2,1)} %param.14), kind=kOutput, calls=%fused_computation.51 | convolution fusion | flops 3222798336 | bytes 8912896 | tf_op jit(solution)/shard_map/dot_general | solution.py:77
  179.7 1.5 collective-permute-start
  181.3 3.3 %collective-permute-start.1 = (bf16[512,512]{0,1:T(8,128)(2,1)S(1)}, bf16[512,512]{0,1:T(8,128)(2,1)S(1)}, u32[]{:S(2)}, u32[]{:S(2)}) collective-permute-start(bf16[512,512]{0,1:T(8,128)(2,1)S(1)} %bitcast.97), channel_id=1, source_target_pairs={{4,0},{8,4},{12,8},{16,12},{20,16},{24,20},{28,24},{0,28},{5,1},{9... | collective-permute-start | bytes 1572872 | tf_op jit(solution)/shard_map/ppermute | solution.py:21
  184.8 1.1 slice_bitcast_fusion.2
  185.9 18.2 %collective-permute-done = bf16[512,512]{0,1:T(8,128)(2,1)S(1)} collective-permute-done((bf16[512,512]{0,1:T(8,128)(2,1)S(1)}, bf16[512,512]{0,1:T(8,128)(2,1)S(1)}, u32[]{:S(2)}, u32[]{:S(2)}) %collective-permute-start) | collective-permute-done | bytes 524320 | tf_op jit(solution)/shard_map/ppermute | solution.py:20
  204.1 2.2 collective-permute-done.1
  206.6 1.4 slice_bitcast_fusion
  208.1 1.1 broadcast.125
  209.1 58.0 %while.25 = (s32[]{:T(128)}, bf16[4,512,4,64]{1,3,2,0:T(8,128)(2,1)}, s32[4]{0:T(128)S(1)}, bf16[3072,4,64]{0,2,1:T(8,128)(2,1)}, s32[2048]{0:T(1024)S(1)}, /*in...) while((s32[]{:T(128)}, ...), condition=%wide.region_11.12_spmd, body=%wide.region_8.11_spmd.sunk | while | flops 550110208 | bytes 19434436 | solution.py:64
  209.1 0.6 dynamic_slice.142
  210.5 0.4 broadcast_compare_fusion.5
  210.9 7.0 %fusion.128 = (f32[4,512]{1,0:T(4,128)S(1)}, f32[4,512,1024]{2,1,0:T(8,128)}) fusion(pred[512,1024]{1,0:T(8,128)(4,1)S(1)} %broadcast_compare_fusion.5, bf16[3072,4,64]{0,2,1:T(8,128)(2,1)S(1)} %get-tuple-element.436, s32[]{:T(128)S(6)} %select_n.103, bf16[2048,4,64]{0,2,1:T(8,128)(2,1)} %get-tuple-element.435, s32[]{:T(128)S(6)} %select_n.104), kind=kOutput, calls=%fused_computation.94.clone.1 | convolution fusion | flops 276825088 | bytes 9707528 | tf_op jit(solution)/shard_map/while/body/eval_jaxpr/sub | solution.py:59
  217.9 5.7 %fusion.129 = bf16[4,512,4,64]{1,3,2,0:T(8,128)(2,1)} fusion(bf16[4,512,4,64]{1,3,2,0:T(8,128)(2,1)} %get-tuple-element.412, s32[]{:T(128)} %get-tuple-element.411, f32[4,512,1024]{2,1,0:T(8,128)} %get-tuple-element.346, f32[4,512]{1,0:T(4,128)S(1)} %get-tuple-element.347, bf16[3072,4,64]{0,2,1:T(8,128)(2,1)} %get-tuple-element.432, s32[]{:T(128)S(6)} %select_n.103), kind=kOutput, calls=%fused_computation.37.clone.1 | convolution fusion | flops 272760832 | bytes 9183748 | tf_op jit(solution)/shard_map/while/body/eval_jaxpr/hqk,khd->qhd/dot_general | solution.py:61
  223.6 0.6 dynamic_slice.142
  225.0 0.4 broadcast_compare_fusion.5
  225.4 7.0 %fusion.128 = (f32[4,512]{1,0:T(4,128)S(1)}, f32[4,512,1024]{2,1,0:T(8,128)}) fusion(pred[512,1024]{1,0:T(8,128)(4,1)S(1)} %broadcast_compare_fusion.5, bf16[3072,4,64]{0,2,1:T(8,128)(2,1)S(1)} %get-tuple-element.436, s32[]{:T(128)S(6)} %select_n.103, bf16[2048,4,64]{0,2,1:T(8,128)(2,1)} %get-tuple-element.435, s32[]{:T(128)S(6)} %select_n.104), kind=kOutput, calls=%fused_computation.94.clone.1 | convolution fusion | flops 276825088 | bytes 9707528 | tf_op jit(solution)/shard_map/while/body/eval_jaxpr/sub | solution.py:59
  232.4 5.7 %fusion.129 = bf16[4,512,4,64]{1,3,2,0:T(8,128)(2,1)} fusion(bf16[4,512,4,64]{1,3,2,0:T(8,128)(2,1)} %get-tuple-element.412, s32[]{:T(128)} %get-tuple-element.411, f32[4,512,1024]{2,1,0:T(8,128)} %get-tuple-element.346, f32[4,512]{1,0:T(4,128)S(1)} %get-tuple-element.347, bf16[3072,4,64]{0,2,1:T(8,128)(2,1)} %get-tuple-element.432, s32[]{:T(128)S(6)} %select_n.103), kind=kOutput, calls=%fused_computation.37.clone.1 | convolution fusion | flops 272760832 | bytes 9183748 | tf_op jit(solution)/shard_map/while/body/eval_jaxpr/hqk,khd->qhd/dot_general | solution.py:61
  238.2 0.6 dynamic_slice.142
  239.5 0.4 broadcast_compare_fusion.5
  239.9 7.0 %fusion.128 = (f32[4,512]{1,0:T(4,128)S(1)}, f32[4,512,1024]{2,1,0:T(8,128)}) fusion(pred[512,1024]{1,0:T(8,128)(4,1)S(1)} %broadcast_compare_fusion.5, bf16[3072,4,64]{0,2,1:T(8,128)(2,1)S(1)} %get-tuple-element.436, s32[]{:T(128)S(6)} %select_n.103, bf16[2048,4,64]{0,2,1:T(8,128)(2,1)} %get-tuple-element.435, s32[]{:T(128)S(6)} %select_n.104), kind=kOutput, calls=%fused_computation.94.clone.1 | convolution fusion | flops 276825088 | bytes 9707528 | tf_op jit(solution)/shard_map/while/body/eval_jaxpr/sub | solution.py:59
  246.9 5.7 %fusion.129 = bf16[4,512,4,64]{1,3,2,0:T(8,128)(2,1)} fusion(bf16[4,512,4,64]{1,3,2,0:T(8,128)(2,1)} %get-tuple-element.412, s32[]{:T(128)} %get-tuple-element.411, f32[4,512,1024]{2,1,0:T(8,128)} %get-tuple-element.346, f32[4,512]{1,0:T(4,128)S(1)} %get-tuple-element.347, bf16[3072,4,64]{0,2,1:T(8,128)(2,1)} %get-tuple-element.432, s32[]{:T(128)S(6)} %select_n.103), kind=kOutput, calls=%fused_computation.37.clone.1 | convolution fusion | flops 272760832 | bytes 9183748 | tf_op jit(solution)/shard_map/while/body/eval_jaxpr/hqk,khd->qhd/dot_general | solution.py:61
  252.7 0.6 dynamic_slice.142
  254.0 0.4 broadcast_compare_fusion.5
  254.4 7.0 %fusion.128 = (f32[4,512]{1,0:T(4,128)S(1)}, f32[4,512,1024]{2,1,0:T(8,128)}) fusion(pred[512,1024]{1,0:T(8,128)(4,1)S(1)} %broadcast_compare_fusion.5, bf16[3072,4,64]{0,2,1:T(8,128)(2,1)S(1)} %get-tuple-element.436, s32[]{:T(128)S(6)} %select_n.103, bf16[2048,4,64]{0,2,1:T(8,128)(2,1)} %get-tuple-element.435, s32[]{:T(128)S(6)} %select_n.104), kind=kOutput, calls=%fused_computation.94.clone.1 | convolution fusion | flops 276825088 | bytes 9707528 | tf_op jit(solution)/shard_map/while/body/eval_jaxpr/sub | solution.py:59
  261.4 5.7 %fusion.129 = bf16[4,512,4,64]{1,3,2,0:T(8,128)(2,1)} fusion(bf16[4,512,4,64]{1,3,2,0:T(8,128)(2,1)} %get-tuple-element.412, s32[]{:T(128)} %get-tuple-element.411, f32[4,512,1024]{2,1,0:T(8,128)} %get-tuple-element.346, f32[4,512]{1,0:T(4,128)S(1)} %get-tuple-element.347, bf16[3072,4,64]{0,2,1:T(8,128)(2,1)} %get-tuple-element.432, s32[]{:T(128)S(6)} %select_n.103), kind=kOutput, calls=%fused_computation.37.clone.1 | convolution fusion | flops 272760832 | bytes 9183748 | tf_op jit(solution)/shard_map/while/body/eval_jaxpr/hqk,khd->qhd/dot_general | solution.py:61
  267.2 3.5 %all-to-all-start.1 = ((bf16[4,512,256]{1,2,0:T(8,128)(2,1)}), bf16[4,512,256]{1,2,0:T(8,128)(2,1)S(1)}, u32[]{:S(2)}, u32[]{:S(2)}) async-start(bf16[4,512,256]{1,2,0:T(8,128)(2,1)} %bitcast.30), calls=%async_computation.1 | async-start | bytes 2097152 | tf_op jit(solution)/shard_map/all_to_all | solution.py:108
  270.7 14.4 %all-to-all-done.1 = bf16[4,512,256]{1,2,0:T(8,128)(2,1)S(1)} async-done(((bf16[4,512,256]{1,2,0:T(8,128)(2,1)}), bf16[4,512,256]{1,2,0:T(8,128)(2,1)S(1)}, u32[]{:S(2)}, u32[]{:S(2)}) %all-to-all-start.1) | async-done | bytes 1048608 | tf_op jit(solution)/shard_map/all_to_all | solution.py:108
  285.1 3.9 %fusion.71 = bf16[512,1024]{1,0:T(8,128)(2,1)} fusion(bf16[512,1024]{1,0:T(8,128)(2,1)S(1)} %get-tuple-element.247, bf16[512,1024]{0,1:T(8,128)(2,1)S(1)} %bitcast.94, bf16[1,1024,1024]{2,1,0:T(8,128)(2,1)} %all-gather.14.cloned.1.call-done), kind=kOutput, calls=%fused_computation.71 | convolution fusion | flops 1075314688 | bytes 5242880 | tf_op jit(solution)/shard_map/dot_general | solution.py:109
  (52 shorter events, 2.1 us)
Async XLA Ops:
  6.5 1.2 copy-start
  6.5 42.7 %all-gather.8.cloned.1.call-start = ((), (), s32[]{:S(2)}) async-start(), calls=%async_computation.2 | async-start | bytes 5242880 | tf_op jit(solution)/shard_map/all_gather | solution.py:78
  7.8 2.7 copy-start.3
  9.8 2.1 copy-start.2
  10.5 2.6 copy-start.4
  11.9 108.1 %all-gather.12.cloned.1.call-start = ((), (), s32[]{:S(2)}) async-start(), calls=%async_computation.4 | async-start | bytes 2621440 | tf_op jit(solution)/shard_map/all_gather | solution.py:111
  116.2 17.9 %all-to-all-start = ((bf16[4,512,256]{1,2,0:T(8,128)(2,1)}), bf16[4,512,256]{1,2,0:T(8,128)(2,1)S(1)}, u32[]{:S(2)}, u32[]{:S(2)}) async-start(bf16[4,512,256]{1,2,0:T(8,128)(2,1)} %bitcast.16), calls=%async_computation | async-start | bytes 2097152 | tf_op jit(solution)/shard_map/all_to_all | solution.py:108
  119.7 53.8 %all-gather.10.cloned.1.call-start = ((), (), s32[]{:S(2)}) async-start(), calls=%async_computation.3 | async-start | bytes 5242880 | tf_op jit(solution)/shard_map/all_gather | solution.py:78
  138.9 131.8 %all-gather.14.cloned.1.call-start = ((), (), s32[]{:S(2)}) async-start(), calls=%async_computation.5 | async-start | bytes 2621440 | tf_op jit(solution)/shard_map/all_gather | solution.py:111
  139.0 45.6 %collective-permute-start.2 = (bf16[512]{0:T(512)(128)(2,1)S(1)}, bf16[512]{0:T(512)(128)(2,1)S(1)}, u32[]{:S(2)}, u32[]{:S(2)}) collective-permute-start(bf16[512]{0:T(512)(128)(2,1)S(1)} %get-tuple-element.244), channel_id=1, source_target_pairs={{0,4},{4,8},{8,12},{12,16},{16,20},{20,24},{24,28},{28,0},{1,5},{5... | collective-permute-start | bytes 3080 | tf_op jit(solution)/shard_map/ppermute | solution.py:20
  140.5 44.1 %collective-permute-start.3 = (bf16[512]{0:T(512)(128)(2,1)S(1)}, bf16[512]{0:T(512)(128)(2,1)S(1)}, u32[]{:S(2)}, u32[]{:S(2)}) collective-permute-start(bf16[512]{0:T(512)(128)(2,1)S(1)} %get-tuple-element.245), channel_id=1, source_target_pairs={{4,0},{8,4},{12,8},{16,12},{20,16},{24,20},{28,24},{0,28},{5,1},{9... | collective-permute-start | bytes 3080 | tf_op jit(solution)/shard_map/ppermute | solution.py:21
  179.7 24.3 %collective-permute-start = (bf16[512,512]{0,1:T(8,128)(2,1)S(1)}, bf16[512,512]{0,1:T(8,128)(2,1)S(1)}, u32[]{:S(2)}, u32[]{:S(2)}) collective-permute-start(bf16[512,512]{0,1:T(8,128)(2,1)S(1)} %bitcast.98), channel_id=1, source_target_pairs={{0,4},{4,8},{8,12},{12,16},{16,20},{20,24},{24,28},{28,0},{1,5},{5... | collective-permute-start | bytes 1572872 | tf_op jit(solution)/shard_map/ppermute | solution.py:20
  181.3 25.0 %collective-permute-start.1 = (bf16[512,512]{0,1:T(8,128)(2,1)S(1)}, bf16[512,512]{0,1:T(8,128)(2,1)S(1)}, u32[]{:S(2)}, u32[]{:S(2)}) collective-permute-start(bf16[512,512]{0,1:T(8,128)(2,1)S(1)} %bitcast.97), channel_id=1, source_target_pairs={{4,0},{8,4},{12,8},{16,12},{20,16},{24,20},{28,24},{0,28},{5,1},{9... | collective-permute-start | bytes 1572872 | tf_op jit(solution)/shard_map/ppermute | solution.py:21
  267.2 17.9 %all-to-all-start.1 = ((bf16[4,512,256]{1,2,0:T(8,128)(2,1)}), bf16[4,512,256]{1,2,0:T(8,128)(2,1)S(1)}, u32[]{:S(2)}, u32[]{:S(2)}) async-start(bf16[4,512,256]{1,2,0:T(8,128)(2,1)} %bitcast.30), calls=%async_computation.1 | async-start | bytes 2097152 | tf_op jit(solution)/shard_map/all_to_all | solution.py:108
  285.1 3.9 %copy-start.1 = (bf16[512,1024]{1,0:T(8,128)(2,1)S(1)}, bf16[512,1024]{1,0:T(8,128)(2,1)}, u32[]{:S(2)}) copy-start(bf16[512,1024]{1,0:T(8,128)(2,1)} %param.10) | copy-start | bytes 3145732
Sparse Core Ops, SparseCore 0:
  12.0 37.1 all-gather.7
  50.8 22.5 all-gather.11
  139.0 34.4 all-gather.9
  174.9 22.5 all-gather.13
where the time goes:
time: 296 us
  matrix products  121 us (41%)
  waiting for transfers between devices  109 us (37%)
  starting transfers between devices  16.9 us (6%)
  local copies, waits for them, and re-layouts  15.9 us (5%)
  between operations  13.3 us (4%)
  other arithmetic  7.79 us (3%)
  blocking collectives  6.2 us (2%)
  loops' own time  5.57 us (2%)
    all_gather x2, waiting for transfers between devices, on_device(): lax.all_gather(normed, 'head', axis=0, tiled=True)  59.7 us
    sub x8, matrix products, one_block(): expo = jnp.exp(scores - row_max)  56.2 us
    dot_general x8, matrix products, one_block(): jnp.einsum('hqk,khd->qhd', probs, value_block, preferred_element_type=jnp...  45.9 us
    all_to_all x2, waiting for transfers between devices, on_device(): lax.all_to_all(attended, 'head', split_axis=0, concat_axis=1, tiled=True)  28.5 us
    ppermute x2, waiting for transfers between devices, extended(): before = lax.ppermute(last, axis, up)  18.2 us
    dot_general x2, matrix products, on_device(): jnp.dot(lax.all_gather(normed, 'head', axis=0, tiled=True), weights_here,...  12.3 us
    all_to_all x2, starting transfers between devices, on_device(): lax.all_to_all(attended, 'head', split_axis=0, concat_axis=1, tiled=True)  7.03 us
    dot_general x2, matrix products, on_device(): jnp.dot(heads_rows, lax.all_gather(w_out[layer_index], 'head', axis=0, ti...  6.86 us
  transfers between devices with their start and end apart: 10, of which 6 were waited for; matrix products, arithmetic and copies ran while one was open for 44% of the time, Pallas kernels for 0%

commit v1 on v0

v1 whole, which is shorter than its diff:
```python
import functools

import jax
import jax.numpy as jnp
from jax import lax
from jax.experimental import pallas as pl
from jax.experimental.pallas import tpu as pltpu
from jax.sharding import PartitionSpec as P

HEAD_DIM = 64
PATCH = 1024


EPSILON = 1e-05


def extended(array, sides, width):
    for axis, dim in sides:
        peers, length = (lax.axis_size(axis), array.shape[dim])
        up = [(i, (i + 1) % peers) for i in range(peers)]
        down = [(j, i) for i, j in up]
        last = lax.slice_in_dim(array, length - width, length, axis=dim)
        first = lax.slice_in_dim(array, 0, width, axis=dim)
        before = lax.ppermute(last, axis, up)
        after = lax.ppermute(first, axis, down)
        array = jnp.concatenate([before, array, after], axis=dim)
    return array


def layer_norm(rows, gain):
    values = rows.astype(jnp.float32)
    center = values - jnp.mean(values, axis=-1, keepdims=True)
    spread = jnp.mean(center * center, axis=-1, keepdims=True)
    return (center * lax.rsqrt(spread + EPSILON) * gain).astype(jnp.bfloat16)


def attend_block(heads_local, kv_stride, k_at, q_ref, kv_ref, qt_ref, kt_ref, out_ref):
    rows = q_ref.shape[0]
    keys = kv_ref.shape[0]
    bias = jnp.where(qt_ref[...] == kt_ref[...], 0.0, -jnp.inf)
    ones = jnp.ones((keys, HEAD_DIM), jnp.bfloat16)
    for head in range(heads_local):
        q_at = head * 3 * HEAD_DIM
        key_at = head * kv_stride + k_at
        query = q_ref[:, q_at : q_at + HEAD_DIM] * jnp.bfloat16(HEAD_DIM ** (-0.5))
        key = kv_ref[:, key_at : key_at + HEAD_DIM]
        value = kv_ref[:, key_at + HEAD_DIM : key_at + 2 * HEAD_DIM]
        scores = lax.dot_general(
            query, key, (((1,), (1,)), ((), ())), preferred_element_type=jnp.float32
        ) + bias
        row_max = jnp.max(scores, axis=-1, keepdims=True)
        expo = jnp.exp(scores - row_max).astype(jnp.bfloat16)
        result = jnp.dot(
            expo, jnp.concatenate([value, ones], axis=1), preferred_element_type=jnp.float32
        )
        normal = result[:, :HEAD_DIM] / result[:, HEAD_DIM : HEAD_DIM + 1]
        out_ref[:, head * HEAD_DIM : (head + 1) * HEAD_DIM] = normal.astype(jnp.bfloat16)


def attend(queries, kv, query_tags, key_tags, kv_stride, k_at, centred):
    block_rows = PATCH // 2
    span, width = queries.shape
    heads_local = width // (3 * HEAD_DIM)
    shift = 1 if centred else 0
    return pl.pallas_call(
        functools.partial(attend_block, heads_local, kv_stride, k_at),
        grid=(span // block_rows,),
        out_shape=jax.ShapeDtypeStruct((span, heads_local * HEAD_DIM), jnp.bfloat16),
        in_specs=[
            pl.BlockSpec((block_rows, width), lambda i: (i, 0)),
            pl.BlockSpec((PATCH, kv.shape[1]), lambda i: ((i + shift) // 2, 0)),
            pl.BlockSpec((block_rows, 1), lambda i: (i, 0)),
            pl.BlockSpec((1, PATCH), lambda i: (0, (i + shift) // 2)),
        ],
        out_specs=pl.BlockSpec((block_rows, heads_local * HEAD_DIM), lambda i: (i, 0)),
        cost_estimate=pl.CostEstimate(
            flops=4 * span * PATCH * heads_local * HEAD_DIM,
            bytes_accessed=span * width * 8,
            transcendentals=span * PATCH * heads_local,
        ),
    )(queries, kv, query_tags.reshape(-1, 1), key_tags.reshape(1, -1))


def on_device(points, order, scan_ids, ln_gain, w_qkv, w_out):
    stream = points[order[0]]
    range_ids = lax.all_gather(scan_ids, "head", axis=0, tiled=True)
    span_rows = range_ids.shape[0]
    heads_local = w_qkv.shape[2] // (3 * HEAD_DIM)
    half_patch = PATCH // 2
    for layer_index in range(2):
        normed = layer_norm(stream, ln_gain[layer_index])
        weights_here = w_qkv[layer_index]
        qkv_span = jnp.dot(
            lax.all_gather(normed, "head", axis=0, tiled=True),
            weights_here,
            preferred_element_type=jnp.float32,
        ).astype(jnp.bfloat16)
        if layer_index == 0:
            attended = attend(
                qkv_span, qkv_span, range_ids, range_ids, 3 * HEAD_DIM, HEAD_DIM, False
            )
        else:
            tags_float = range_ids.astype(jnp.bfloat16)
            kv_flat = qkv_span.reshape(span_rows, heads_local, 3, HEAD_DIM)[:, :, 1:].reshape(
                span_rows, heads_local * 2 * HEAD_DIM
            )
            wide_kv, wide_tags = (
                extended(kv_flat, (("curve", 0),), half_patch),
                extended(tags_float, (("curve", 0),), half_patch),
            )
            attended = attend(
                qkv_span,
                wide_kv,
                range_ids,
                wide_tags.astype(jnp.int32),
                2 * HEAD_DIM,
                0,
                True,
            )
        heads_rows = lax.all_to_all(attended, "head", split_axis=0, concat_axis=1, tiled=True)
        update = jnp.dot(
            heads_rows,
            lax.all_gather(w_out[layer_index], "head", axis=0, tiled=True),
            preferred_element_type=jnp.float32,
        )
        stream = (stream.astype(jnp.float32) + update).astype(jnp.bfloat16)
    return stream


def solution(mesh):
    in_specs = (
        P(("curve", "head"), None),
        P(("curve", "head"), None),
        P(("curve", "head")),
        P(),
        P(None, None, "head"),
        P(None, "head", None),
    )
    out_specs = P(("curve", "head"), None)
    return jax.shard_map(
        on_device, mesh=mesh, in_specs=in_specs, out_specs=out_specs, check_vma=False
    )
```

time: 296 us -> 234 us (0.79)
  matrix products: 121 us -> 22.4 us
  Pallas kernels: 0 us -> 35.3 us
  local copies, waits for them, and re-layouts: 15.9 us -> 24.6 us
  loops' own time: 5.57 us -> 0 us
    sub x8 -> x0, matrix products: 56.2 us -> none  [one_block(): expo = jnp.exp(scores - row_max)]
    dot_general x8 -> x0, matrix products: 45.9 us -> none  [one_block(): jnp.einsum('hqk,khd->qhd', probs, value_block, preferred_element_type=jnp...]
    pallas_call x0 -> x2, Pallas kernels: none -> 35.3 us  [attend(): pl.pallas_call(functools.partial(attend_block, heads_local, kv_stride, k_...]
    ppermute x2, waiting for transfers between devices: 18.2 us -> 0.01 us  [extended(): before = lax.ppermute(last, axis, up)]
    ppermute x2, waiting for transfers between devices: 2.2 us -> 15.6 us  [extended(): after = lax.ppermute(first, axis, down)]
    another operation x2 -> x0, loops' own time: 5.57 us -> none  [attend(): outputs = lax.map(one_block, jnp.arange(blocks_count))]
    dynamic_slice x24 -> x0, local copies, waits for them, and re-layouts: 5.54 us -> none  [the longest x8 4.84 us: attend(): outputs = lax.map(one_block, jnp.arange(blocks_count))]
    convert_element_type x0 -> x1, local copies, waits for them, and re-layouts: none -> 4.75 us  [on_device(): qkv_span = jnp.dot(lax.all_gather(normed, 'head', axis=0, tiled=True), we...]
  transfers between devices with their start and end apart: 10 -> 10, of which waited for: 6 -> 5; matrix products, arithmetic and copies ran while one was open for 44% -> 17% of each run, Pallas kernels for 0% -> 15%
where the time goes in v1:
time: 234 us
  waiting for transfers between devices  107 us (46%)
  Pallas kernels  35.3 us (15%)
  local copies, waits for them, and re-layouts  24.6 us (11%)
  matrix products  22.4 us (10%)
  starting transfers between devices  16.3 us (7%)
  between operations  13.3 us (6%)
  other arithmetic  7.98 us (3%)
  blocking collectives  6.2 us (3%)
    all_gather x2, waiting for transfers between devices, on_device(): lax.all_gather(normed, 'head', axis=0, tiled=True)  62.7 us
    pallas_call x2, Pallas kernels, attend(): pl.pallas_call(functools.partial(attend_block, heads_local, kv_stride, k_...  35.3 us
    all_to_all x2, waiting for transfers between devices, on_device(): lax.all_to_all(attended, 'head', split_axis=0, concat_axis=1, tiled=True)  28.7 us
    dot_general x2, matrix products, on_device(): jnp.dot(lax.all_gather(normed, 'head', axis=0, tiled=True), weights_here,...  15.6 us
    ppermute x2, waiting for transfers between devices, extended(): after = lax.ppermute(first, axis, down)  15.6 us
    ppermute x2, starting transfers between devices, extended(): after = lax.ppermute(first, axis, down)  9 us
    all_to_all x2, starting transfers between devices, on_device(): lax.all_to_all(attended, 'head', split_axis=0, concat_axis=1, tiled=True)  7.03 us
    dot_general x2, matrix products, on_device(): jnp.dot(heads_rows, lax.all_gather(w_out[layer_index], 'head', axis=0, ti...  6.82 us
  transfers between devices with their start and end apart: 10, of which 5 were waited for; matrix products, arithmetic and copies ran while one was open for 17% of the time, Pallas kernels for 15%

profile of v1, /device:TPU:0, one launch (start us, length us, event | category | flops | bytes accessed | tf_op | source)
XLA Modules:
  0.0 233.6 jit_solution(2070810661206250517)
XLA Ops:
  6.5 0.0 copy-start
  6.5 0.0 all-gather.8.cloned.1.call-start
  6.5 0.8 compare_select_fusion
  7.3 0.8 fusion.26
  8.1 0.0 copy-done
  8.1 2.1 gather_fusion
  10.2 0.2 convert_reduce_fusion.1
  10.4 0.0 copy-start.3
  10.4 0.4 fusion.7
  10.8 1.4 fusion.9
  12.2 0.0 copy-start.6
  12.2 0.0 all-gather.8.cloned.1.call-update
  12.2 0.0 all-gather.12.cloned.1.call-start
  12.3 0.0 copy-done.3
  12.3 1.0 fusion.25
  13.3 0.0 all-gather.12.cloned.1.call-update
  13.4 0.0 copy-done.6
  13.4 6.2 %all-gather.2 = s32[4,1,512]{2,1,0:T(1,128)S(1)} all-gather(s32[1,1,512]{2,1,0:T(1,128)S(1)} %bitcast.58), channel_id=1, replica_groups=mesh['curve'=8,'head'=4] {'head'}, dimensions={0}, use_global_device_ids=true | all-gather | bytes 10240 | tf_op jit(solution)/shard_map/all_gather | solution.py:86
  19.6 0.0 copy-start.4
  19.6 1.4 copy.17.qt_ref
  20.9 28.6 %all-gather.8.cloned.1.call-done = bf16[2048,1024]{1,0:T(8,128)(2,1)} async-done(((bf16[512,1024]{1,0:T(8,128)(2,1)}), bf16[2048,1024]{1,0:T(8,128)(2,1)}) %all-gather.8.cloned.1.call-update) | async-done | bytes 4194320 | tf_op jit(solution)/shard_map/all_gather | solution.py:94
  49.6 7.8 %convolution_convert_fusion.1.q_ref.kv_ref = bf16[2048,768]{1,0:T(8,128)(2,1)} fusion(bf16[2048,1024]{1,0:T(8,128)(2,1)} %all-gather.8.cloned.1.call-done, bf16[2,1024,768]{2,1,0:T(8,128)(2,1)} %param.10), kind=kOutput, calls=%fused_computation.2 | convolution fusion | flops 3222798336 | bytes 8912896 | tf_op jit(solution)/shard_map/dot_general | solution.py:93
  57.4 0.0 copy-done.4
  57.4 18.1 %shard_map.64 = bf16[2048,256]{1,0:T(8,128)(2,1)} custom-call(bf16[2048,768]{1,0:T(8,128)(2,1)} %convolution_convert_fusion.1.q_ref.kv_ref, bf16[2048,768]{1,0:T(8,128)(2,1)} %convolution_convert_fusion.1.q_ref.kv_ref, s32[2048,1]{1,0:T(8,128)} %copy.17.qt_ref, s32[1,2048]{1,0:T(1,128)} %bitcast.53), custom_call_target="tpu_custom_call" | custom-call | flops 2147483648 | bytes 12582912 | tf_op jit(solution)/shard_map/pallas_call | solution.py:65
  75.5 2.3 copy.18
  77.8 3.5 %all-to-all-start = ((bf16[4,512,256]{1,2,0:T(8,128)(2,1)}), bf16[4,512,256]{1,2,0:T(8,128)(2,1)S(1)}, u32[]{:S(2)}, u32[]{:S(2)}) async-start(bf16[4,512,256]{1,2,0:T(8,128)(2,1)} %copy.18), calls=%async_computation | async-start | bytes 2097152 | tf_op jit(solution)/shard_map/all_to_all | solution.py:120
  81.3 0.0 all-gather.10.cloned.1.call-start
  81.4 0.0 all-gather.12.cloned.1.call-done
  81.4 14.3 %all-to-all-done = bf16[4,512,256]{1,2,0:T(8,128)(2,1)S(1)} async-done(((bf16[4,512,256]{1,2,0:T(8,128)(2,1)}), bf16[4,512,256]{1,2,0:T(8,128)(2,1)S(1)}, u32[]{:S(2)}, u32[]{:S(2)}) %all-to-all-start) | async-done | bytes 1048608 | tf_op jit(solution)/shard_map/all_to_all | solution.py:120
  95.7 3.0 %convert_reduce_fusion = (f32[512]{0:T(512)S(1)}, bf16[512,1024]{1,0:T(8,128)(2,1)S(1)}) fusion(bf16[512,1024]{0,1:T(8,128)(2,1)S(1)} %bitcast.48, bf16[1,1024,1024]{2,1,0:T(8,128)(2,1)} %all-gather.12.cloned.1.call-done, bf16[512,1024]{1,0:T(8,128)(2,1)S(1)} %gather_fusion), kind=kOutput, calls=%fused_computation.6 | convolution fusion | flops 1076362752 | bytes 5244928 | tf_op jit(solution)/shard_map/dot_general | solution.py:121
  98.7 0.0 copy-start.1
  98.7 0.4 fusion.4
  99.1 0.5 copy-done.1
  99.7 1.3 fusion.6
  101.0 0.0 all-gather.10.cloned.1.call-update
  101.0 0.2 all-gather.14.cloned.1.call-start
  101.3 0.3 all-gather.14.cloned.1.call-update
  101.6 34.0 %all-gather.10.cloned.1.call-done = bf16[2048,1024]{1,0:T(8,128)(2,1)} async-done(((bf16[512,1024]{1,0:T(8,128)(2,1)}), bf16[2048,1024]{1,0:T(8,128)(2,1)}) %all-gather.10.cloned.1.call-update) | async-done | bytes 4194320 | tf_op jit(solution)/shard_map/all_gather | solution.py:94
  135.6 7.8 %convolution_convert_fusion.q_ref = bf16[2048,768]{1,0:T(8,128)(2,1)} fusion(bf16[2048,1024]{1,0:T(8,128)(2,1)} %all-gather.10.cloned.1.call-done, bf16[2,1024,768]{2,1,0:T(8,128)(2,1)} %param.10), kind=kOutput, calls=%fused_computation.1 | convolution fusion | flops 3222798336 | bytes 8912896 | tf_op jit(solution)/shard_map/dot_general | solution.py:93
  143.5 4.7 %copy.20 = bf16[2048,768]{0,1:T(8,128)(2,1)} copy(bf16[2048,768]{1,0:T(8,128)(2,1)} %convolution_convert_fusion.q_ref) | data formatting | bytes 6291456 | tf_op jit(solution)/shard_map/convert_element_type | solution.py:97
  148.2 0.0 copy-start.5
  148.2 1.3 fusion.24
  149.5 1.0 copy.22
  150.6 4.2 %collective-permute-start.1 = (bf16[512,512]{1,0:T(8,128)(2,1)}, bf16[512,512]{1,0:T(8,128)(2,1)}, u32[]{:S(2)}, u32[]{:S(2)}) collective-permute-start(bf16[512,512]{1,0:T(8,128)(2,1)} %copy.22), channel_id=1, source_target_pairs={{4,0},{8,4},{12,8},{16,12},{20,16},{24,20},{28,24},{0,28},{5,1},{9... | collective-permute-start | bytes 1572872 | tf_op jit(solution)/shard_map/ppermute | solution.py:25
  154.8 1.0 copy.21
  155.8 0.0 collective-permute-start
  155.8 0.0 copy-done.5
  155.8 4.8 %collective-permute-start.3 = (bf16[512]{0:T(512)(128)(2,1)S(1)}, bf16[512]{0:T(512)(128)(2,1)S(1)}, u32[]{:S(2)}, u32[]{:S(2)}) collective-permute-start(bf16[512]{0:T(512)(128)(2,1)S(1)} %get-tuple-element.6), channel_id=1, source_target_pairs={{4,0},{8,4},{12,8},{16,12},{20,16},{24,20},{28,24},{0,28},{5,1},{9... | collective-permute-start | bytes 3080 | tf_op jit(solution)/shard_map/ppermute | solution.py:25
  160.6 0.0 collective-permute-start.2
  160.6 15.6 %collective-permute-done.3 = bf16[512]{0:T(512)(128)(2,1)S(1)} collective-permute-done((bf16[512]{0:T(512)(128)(2,1)S(1)}, bf16[512]{0:T(512)(128)(2,1)S(1)}, u32[]{:S(2)}, u32[]{:S(2)}) %collective-permute-start.3) | collective-permute-done | bytes 1056 | tf_op jit(solution)/shard_map/ppermute | solution.py:25
  176.2 0.0 collective-permute-done.2
  176.2 0.6 maximum_convert_fusion.kt_ref
  176.8 3.2 %slice.59 = bf16[2048,4,2,64]{0,3,2,1:T(8,128)(2,1)} slice(bf16[2048,4,3,64]{0,3,2,1:T(8,128)(2,1)} %bitcast.44), slice={[0:2048], [0:4], [1:3], [0:64]} | slice | bytes 4194304 | tf_op jit(solution)/shard_map/slice | solution.py:104
  180.0 2.9 %copy.23 = bf16[2048,512]{1,0:T(8,128)(2,1)S(1)} copy(bf16[2048,512]{0,1:T(8,128)(2,1)} %bitcast.45) | data formatting | bytes 4194304 | tf_op jit(solution)/shard_map/reshape | solution.py:104
  182.9 0.0 collective-permute-done.1
  182.9 0.0 collective-permute-done
  182.9 2.8 %pad_maximum_fusion.kv_ref = bf16[3072,512]{1,0:T(8,128)(2,1)} fusion(bf16[512,512]{1,0:T(8,128)(2,1)} %collective-permute-done.1, bf16[2048,512]{1,0:T(8,128)(2,1)S(1)} %copy.23, bf16[512,512]{1,0:T(8,128)(2,1)} %collective-permute-done), kind=kLoop, calls=%fused_computation.3 | loop fusion | flops 9437184 | bytes 6291456 | tf_op jit(solution)/shard_map/concatenate | solution.py:26
  185.7 17.2 %shard_map.65 = bf16[2048,256]{1,0:T(8,128)(2,1)} custom-call(bf16[2048,768]{1,0:T(8,128)(2,1)} %convolution_convert_fusion.q_ref, bf16[3072,512]{1,0:T(8,128)(2,1)} %pad_maximum_fusion.kv_ref, s32[2048,1]{1,0:T(8,128)} %copy.17.qt_ref, s32[1,3072]{1,0:T(1,128)} %maximum_convert_fusion.kt_ref), custom_call_target="tpu_custom_call" | custom-call | flops 2147483648 | bytes 12582912 | tf_op jit(solution)/shard_map/pallas_call | solution.py:65
  202.9 2.4 %copy.25 = bf16[4,512,256]{1,2,0:T(8,128)(2,1)} copy(bf16[4,512,256]{2,1,0:T(8,128)(2,1)} %bitcast.50) | data formatting | bytes 2097152 | tf_op jit(solution)/shard_map/all_to_all | solution.py:120
  205.3 3.5 %all-to-all-start.1 = ((bf16[4,512,256]{1,2,0:T(8,128)(2,1)}), bf16[4,512,256]{1,2,0:T(8,128)(2,1)S(1)}, u32[]{:S(2)}, u32[]{:S(2)}) async-start(bf16[4,512,256]{1,2,0:T(8,128)(2,1)} %copy.25), calls=%async_computation.1 | async-start | bytes 2097152 | tf_op jit(solution)/shard_map/all_to_all | solution.py:120
  208.8 0.0 all-gather.14.cloned.1.call-done
  208.8 14.4 %all-to-all-done.1 = bf16[4,512,256]{1,2,0:T(8,128)(2,1)S(1)} async-done(((bf16[4,512,256]{1,2,0:T(8,128)(2,1)}), bf16[4,512,256]{1,2,0:T(8,128)(2,1)S(1)}, u32[]{:S(2)}, u32[]{:S(2)}) %all-to-all-start.1) | async-done | bytes 1048608 | tf_op jit(solution)/shard_map/all_to_all | solution.py:120
  223.2 0.0 copy-done.2
  223.2 3.8 %fusion.11 = bf16[512,1024]{1,0:T(8,128)(2,1)} fusion(bf16[512,1024]{1,0:T(8,128)(2,1)S(1)} %copy-done.2, bf16[512,1024]{0,1:T(8,128)(2,1)S(1)} %bitcast.49, bf16[1,1024,1024]{2,1,0:T(8,128)(2,1)} %all-gather.14.cloned.1.call-done), kind=kOutput, calls=%fused_computation.21 | convolution fusion | flops 1075314688 | bytes 5242880 | tf_op jit(solution)/shard_map/dot_general | solution.py:121
  (10 shorter events, 0.1 us)
Async XLA Ops:
  6.5 1.6 copy-start
  6.5 43.0 %all-gather.8.cloned.1.call-start = ((), (), s32[]{:S(2)}) async-start(), calls=%async_computation.2 | async-start | bytes 5242880 | tf_op jit(solution)/shard_map/all_gather | solution.py:94
  10.4 1.9 copy-start.3
  12.2 1.2 copy-start.6
  12.2 69.2 %all-gather.12.cloned.1.call-start = ((), (), s32[]{:S(2)}) async-start(), calls=%async_computation.4 | async-start | bytes 2621440 | tf_op jit(solution)/shard_map/all_gather | solution.py:123
  19.6 37.8 %copy-start.4 = (s32[4,1,512]{2,1,0:T(1,128)}, s32[4,1,512]{2,1,0:T(1,128)S(1)}, u32[]{:S(2)}) copy-start(s32[4,1,512]{2,1,0:T(1,128)S(1)} %all-gather.2) | copy-start | bytes 24580
  77.8 17.9 %all-to-all-start = ((bf16[4,512,256]{1,2,0:T(8,128)(2,1)}), bf16[4,512,256]{1,2,0:T(8,128)(2,1)S(1)}, u32[]{:S(2)}, u32[]{:S(2)}) async-start(bf16[4,512,256]{1,2,0:T(8,128)(2,1)} %copy.18), calls=%async_computation | async-start | bytes 2097152 | tf_op jit(solution)/shard_map/all_to_all | solution.py:120
  81.3 54.3 %all-gather.10.cloned.1.call-start = ((), (), s32[]{:S(2)}) async-start(), calls=%async_computation.3 | async-start | bytes 5242880 | tf_op jit(solution)/shard_map/all_gather | solution.py:94
  98.7 1.0 copy-start.1
  101.0 107.8 %all-gather.14.cloned.1.call-start = ((), (), s32[]{:S(2)}) async-start(), calls=%async_computation.5 | async-start | bytes 2621440 | tf_op jit(solution)/shard_map/all_gather | solution.py:123
  148.2 7.6 %copy-start.5 = (s32[4,1,512]{2,1,0:T(1,128)S(1)}, s32[4,1,512]{2,1,0:T(1,128)}, u32[]{:S(2)}) copy-start(s32[4,1,512]{2,1,0:T(1,128)} %copy-done.4) | copy-start | bytes 24580
  150.6 32.3 %collective-permute-start.1 = (bf16[512,512]{1,0:T(8,128)(2,1)}, bf16[512,512]{1,0:T(8,128)(2,1)}, u32[]{:S(2)}, u32[]{:S(2)}) collective-permute-start(bf16[512,512]{1,0:T(8,128)(2,1)} %copy.22), channel_id=1, source_target_pairs={{4,0},{8,4},{12,8},{16,12},{20,16},{24,20},{28,24},{0,28},{5,1},{9... | collective-permute-start | bytes 1572872 | tf_op jit(solution)/shard_map/ppermute | solution.py:25
  155.8 27.1 %collective-permute-start = (bf16[512,512]{1,0:T(8,128)(2,1)}, bf16[512,512]{1,0:T(8,128)(2,1)}, u32[]{:S(2)}, u32[]{:S(2)}) collective-permute-start(bf16[512,512]{1,0:T(8,128)(2,1)} %copy.21), channel_id=1, source_target_pairs={{0,4},{4,8},{8,12},{12,16},{16,20},{20,24},{24,28},{28,0},{1,5},{5... | collective-permute-start | bytes 1572872 | tf_op jit(solution)/shard_map/ppermute | solution.py:24
  155.8 20.4 %collective-permute-start.3 = (bf16[512]{0:T(512)(128)(2,1)S(1)}, bf16[512]{0:T(512)(128)(2,1)S(1)}, u32[]{:S(2)}, u32[]{:S(2)}) collective-permute-start(bf16[512]{0:T(512)(128)(2,1)S(1)} %get-tuple-element.6), channel_id=1, source_target_pairs={{4,0},{8,4},{12,8},{16,12},{20,16},{24,20},{28,24},{0,28},{5,1},{9... | collective-permute-start | bytes 3080 | tf_op jit(solution)/shard_map/ppermute | solution.py:25
  160.6 15.6 %collective-permute-start.2 = (bf16[512]{0:T(512)(128)(2,1)S(1)}, bf16[512]{0:T(512)(128)(2,1)S(1)}, u32[]{:S(2)}, u32[]{:S(2)}) collective-permute-start(bf16[512]{0:T(512)(128)(2,1)S(1)} %get-tuple-element.5), channel_id=1, source_target_pairs={{0,4},{4,8},{8,12},{12,16},{16,20},{20,24},{24,28},{28,0},{1,5},{5... | collective-permute-start | bytes 3080 | tf_op jit(solution)/shard_map/ppermute | solution.py:24
  202.9 20.3 %copy-start.2 = (bf16[512,1024]{1,0:T(8,128)(2,1)S(1)}, bf16[512,1024]{1,0:T(8,128)(2,1)}, u32[]{:S(2)}) copy-start(bf16[512,1024]{1,0:T(8,128)(2,1)} %copy-done.1) | copy-start | bytes 3145732
  205.3 17.9 %all-to-all-start.1 = ((bf16[4,512,256]{1,2,0:T(8,128)(2,1)}), bf16[4,512,256]{1,2,0:T(8,128)(2,1)S(1)}, u32[]{:S(2)}, u32[]{:S(2)}) async-start(bf16[4,512,256]{1,2,0:T(8,128)(2,1)} %copy.25), calls=%async_computation.1 | async-start | bytes 2097152 | tf_op jit(solution)/shard_map/all_to_all | solution.py:120
Sparse Core Ops, SparseCore 0:
  12.3 37.1 all-gather.7
  51.1 22.5 all-gather.11
  101.2 34.4 all-gather.9
  137.1 22.5 all-gather.13

commit v2 on v0

v2 whole, which is shorter than its diff:
```python
import functools

import jax
import jax.numpy as jnp
from jax import lax
from jax.experimental import pallas as pl
from jax.experimental.pallas import tpu as pltpu
from jax.sharding import PartitionSpec as P

HEAD_DIM = 64
PATCH = 1024


EPSILON = 1e-05


def layer_norm(rows, gain):
    values = rows.astype(jnp.float32)
    center = values - jnp.mean(values, axis=-1, keepdims=True)
    spread = jnp.mean(center * center, axis=-1, keepdims=True)
    return (center * lax.rsqrt(spread + EPSILON) * gain).astype(jnp.bfloat16)


def remote(src, dst, send_sem, recv_sem, device):
    return pltpu.make_async_remote_copy(
        src_ref=src,
        dst_ref=dst,
        send_sem=send_sem,
        recv_sem=recv_sem,
        device_id=device,
        device_id_type=pl.DeviceIdType.MESH,
    )


def layer_kernel(
    peers, ranges, halo, x_ref, tag_ref, w_ref, wo_ref, stream_ref, out_ref,
    all_x, q_buf, kv_buf, tags, att, heads, all_wo,
    x_recv, x_send, w_recv, w_send, t_recv, t_send, h_recv, h_send, kv_recv, kv_send,
):
    chunks, chunk_rows, _ = x_ref.shape
    rows = chunks * chunk_rows
    heads_local = w_ref.shape[1] // (3 * HEAD_DIM)
    chips = peers // 2
    window_blocks = PATCH // rows
    curve = lax.axis_index("curve")
    me = lax.axis_index("head")
    chip, core = me // 2, me % 2
    partner = chip * 2 + 1 - core
    up, down = {"curve": (curve + 1) % ranges}, {"curve": (curve + ranges - 1) % ranges}
    same = [((chip + s) % chips) * 2 + core for s in range(chips)]
    other = [((chip + s) % chips) * 2 + 1 - core for s in range(chips)]
    others = [(me + t) % peers for t in range(1, peers)]

    barrier = pltpu.get_barrier_semaphore()
    for blk in others:
        pl.semaphore_signal(
            barrier, inc=1, device_id={"head": blk}, device_id_type=pl.DeviceIdType.MESH
        )
    if halo:
        for neighbour in (up, down):
            pl.semaphore_signal(
                barrier, inc=1, device_id=neighbour, device_id_type=pl.DeviceIdType.MESH
            )
    pl.semaphore_wait(barrier, peers - 1 + (2 if halo else 0))

    def direct_x(s, c):
        dest = partner if s == 0 else same[s]
        return remote(
            x_ref.at[c], all_x.at[me, c], x_send.at[s, c], x_recv.at[me, c], {"head": dest}
        )

    def passed_x(s, c):
        part = all_x.at[same[s], c]
        return remote(
            part, part, x_send.at[chips + s, c], x_recv.at[same[s], c], {"head": partner}
        )

    def wait_x(blk, c):
        part = all_x.at[blk, c]
        remote(part, part, x_send.at[0, c], x_recv.at[blk, c], {"head": partner}).wait_recv()

    def tag_copy(t):
        return remote(
            tag_ref.at[0], tags.at[halo + me], t_send.at[t], t_recv.at[halo + me],
            {"head": others[t]},
        )

    def direct_w(s):
        dest = partner if s == 0 else same[s]
        return remote(wo_ref, all_wo.at[me], w_send.at[s], w_recv.at[me], {"head": dest})

    def passed_w(s):
        part = all_wo.at[same[s]]
        return remote(
            part, part, w_send.at[chips + s], w_recv.at[same[s]], {"head": partner}
        )

    def wait_w(blk):
        part = all_wo.at[blk]
        remote(part, part, w_send.at[0], w_recv.at[blk], {"head": partner}).wait_recv()

    def edge(buffer, send, recv, j):
        if j < halo:
            src, dst, device = buffer.at[peers + j], buffer.at[j], up
        else:
            src, dst, device = buffer.at[j], buffer.at[peers + j], down
        return remote(src, dst, send.at[j], recv.at[j], device)

    tag_send_edge = peers - 1

    for s in range(chips):
        for c in range(chunks):
            direct_x(s, c).start()
    for t in range(peers - 1):
        tag_copy(t).start()
    direct_w(0).start()
    tags[halo + me] = tag_ref[0]

    def project(values, blk, first_row):
        result = jnp.dot(values, w_ref[...], preferred_element_type=jnp.float32)
        result = result.astype(jnp.bfloat16)
        at = pl.ds(first_row, chunk_rows)
        for head in range(heads_local):
            base = head * 3 * HEAD_DIM
            q_buf[blk, at, head * HEAD_DIM : (head + 1) * HEAD_DIM] = result[
                :, base : base + HEAD_DIM
            ] * jnp.bfloat16(HEAD_DIM ** (-0.5))
            kv_buf[halo + blk, at, head * 2 * HEAD_DIM : (head + 1) * 2 * HEAD_DIM] = result[
                :, base + HEAD_DIM : base + 3 * HEAD_DIM
            ]

    def project_block(blk):
        for c in range(chunks):
            project(all_x[blk, c], blk, c * chunk_rows)

    def attend(blk):
        first = (blk + halo) // window_blocks * window_blocks
        column = jnp.transpose(
            jnp.broadcast_to(tags[halo + blk].astype(jnp.float32), (128, rows))
        )[:, :1]
        line = jnp.concatenate(
            [tags[first + j].astype(jnp.float32) for j in range(window_blocks)], axis=1
        )
        bias = jnp.where(column == line, 0.0, -jnp.inf)
        ones = jnp.ones((PATCH, HEAD_DIM), jnp.bfloat16)
        for head in range(heads_local):
            at = head * 2 * HEAD_DIM
            wide = kv_buf[pl.ds(first, window_blocks), :, at : at + 2 * HEAD_DIM].reshape(
                PATCH, 2 * HEAD_DIM
            )
            query = q_buf[blk, :, head * HEAD_DIM : (head + 1) * HEAD_DIM]
            scores = lax.dot_general(
                query, wide[:, :HEAD_DIM], (((1,), (1,)), ((), ())),
                preferred_element_type=jnp.float32,
            ) + bias
            row_max = jnp.max(scores, axis=-1, keepdims=True)
            expo = jnp.exp(scores - row_max).astype(jnp.bfloat16)
            result = jnp.dot(
                expo,
                jnp.concatenate([wide[:, HEAD_DIM:], ones], axis=1),
                preferred_element_type=jnp.float32,
            )
            normal = result[:, :HEAD_DIM] / result[:, HEAD_DIM : HEAD_DIM + 1]
            att[blk, :, head * HEAD_DIM : (head + 1) * HEAD_DIM] = normal.astype(jnp.bfloat16)

    def head_copy(t):
        blk = others[t]
        return remote(
            att.at[blk], heads.at[me], h_send.at[t], h_recv.at[me], {"head": blk}
        )

    def head_copy_to(blk):
        t = (blk - me + peers - 1) % peers
        return remote(
            att.at[blk], heads.at[me], h_send.at[t], h_recv.at[me], {"head": blk}
        )

    for c in range(chunks):
        project(x_ref[c], me, c * chunk_rows)
    for c in range(chunks):
        wait_x(partner, c)
    project_block(partner)
    for blk in others:
        part = tags.at[halo + blk]
        remote(part, part, t_send.at[0], t_recv.at[halo + blk], {"head": partner}).wait_recv()
    if halo:
        for j in range(2 * halo):
            edge(tags, t_send.at[pl.ds(peers, 2 * halo)], t_recv.at[pl.ds(peers + 2 * halo, 2 * halo)], j).start()

    early = not halo and window_blocks == 2
    if early:
        attend(me)
        attend(partner)
        head_copy_to(partner).start()
    for s in range(1, chips):
        for c in range(chunks):
            wait_x(same[s], c)
            passed_x(s, c).start()
            project(all_x[same[s], c], same[s], c * chunk_rows)
    for s in range(1, chips):
        direct_w(s).start()
        for c in range(chunks):
            wait_x(other[s], c)
            project(all_x[other[s], c], other[s], c * chunk_rows)
    if halo:
        for j in range(2 * halo):
            edge(kv_buf, kv_send, kv_recv, j).start()
        middle = chips // 2 if window_blocks == 2 else 0
        for j in range(2 * halo):
            edge(tags, t_send.at[pl.ds(peers, 2 * halo)], t_recv.at[pl.ds(peers + 2 * halo, 2 * halo)], j).wait_recv()

    def finish(blk):
        attend(blk)

        @pl.when(blk != me)
        def _():
            head_copy_to(blk).start()

    if early:
        for s in range(1, chips):
            finish(other[s])
            finish(same[s])
    else:
        if halo:
            inner = list(range(halo, peers - halo))
            outer = list(range(peers - halo, peers)) + list(range(halo))

            def inner_step(i, carry):
                finish(halo + (me + 1 + i) % (peers - 2 * halo))
                return carry

            lax.fori_loop(0, len(inner), inner_step, 0)
            for j in range(2 * halo):
                edge(kv_buf, kv_send, kv_recv, j).wait_recv()

            def outer_step(i, carry):
                finish((peers - halo + (me + i) % (2 * halo)) % peers)
                return carry

            lax.fori_loop(0, len(outer), outer_step, 0)
        else:

            def step(i, carry):
                finish((me + 1 + i) % peers)
                return carry

            lax.fori_loop(0, peers, step, 0)

    wait_w(partner)
    for s in range(1, chips):
        wait_w(same[s])
        passed_w(s).start()
    heads[me] = att[me]
    all_wo[me] = wo_ref[...]
    for s in range(1, chips):
        wait_w(other[s])
    for blk in others:
        part = heads.at[blk]
        remote(part, part, h_send.at[0], h_recv.at[blk], {"head": partner}).wait_recv()

    for c in range(chunks):
        at = pl.ds(c * chunk_rows, chunk_rows)
        total = stream_ref[at, :].astype(jnp.float32)
        for blk in range(peers):
            total += jnp.dot(
                heads[blk, at, :], all_wo[blk], preferred_element_type=jnp.float32
            )
        out_ref[at, :] = total.astype(jnp.bfloat16)

    for s in range(chips):
        for c in range(chunks):
            direct_x(s, c).wait_send()
            if s:
                passed_x(s, c).wait_send()
        direct_w(s).wait_send()
        if s:
            passed_w(s).wait_send()
    for t in range(peers - 1):
        tag_copy(t).wait_send()
        head_copy(t).wait_send()
    for j in range(2 * halo):
        edge(tags, t_send.at[pl.ds(peers, 2 * halo)], t_recv.at[pl.ds(peers + 2 * halo, 2 * halo)], j).wait_send()
        edge(kv_buf, kv_send, kv_recv, j).wait_send()


def layer(index, stream, normed, tag_row, weights, out_weights):
    rows, width = stream.shape
    peers, ranges = lax.axis_size("head"), lax.axis_size("curve")
    halo = PATCH // 2 // rows if index else 0
    chips = peers // 2
    chunks = max(1, rows // 256)
    columns = out_weights.shape[0]
    vmem = pl.BlockSpec(memory_space=pltpu.VMEM)
    dma = pltpu.SemaphoreType.DMA
    bf16 = jnp.bfloat16
    return pl.pallas_call(
        functools.partial(layer_kernel, peers, ranges, halo),
        out_shape=jax.ShapeDtypeStruct((rows, width), bf16),
        in_specs=[vmem] * 5,
        out_specs=vmem,
        scratch_shapes=[
            pltpu.VMEM((peers, chunks, rows // chunks, width), bf16),
            pltpu.VMEM((peers, rows, columns), bf16),
            pltpu.VMEM((peers + 2 * halo, rows, 2 * columns), bf16),
            pltpu.VMEM((peers + 2 * halo, 1, rows), jnp.int32),
            pltpu.VMEM((peers, rows, columns), bf16),
            pltpu.VMEM((peers, rows, columns), bf16),
            pltpu.VMEM((peers, columns, width), bf16),
            dma((peers, chunks)),
            dma((peers, chunks)),
            dma((peers,)),
            dma((peers,)),
            dma((peers + 4 * halo,)),
            dma((peers + 2 * halo,)),
            dma((peers,)),
            dma((peers,)),
            dma((max(1, 2 * halo),)),
            dma((max(1, 2 * halo),)),
        ],
        compiler_params=pltpu.CompilerParams(collective_id=index, has_side_effects=True),
        cost_estimate=pl.CostEstimate(
            flops=20 * rows * width * width, bytes_accessed=20 * rows * width, transcendentals=0
        ),
    )(
        normed.reshape(chunks, rows // chunks, width),
        tag_row,
        weights,
        out_weights,
        stream,
    )


def on_device(points, order, scan_ids, ln_gain, w_qkv, w_out):
    stream = points[order[0]]
    tag_row = scan_ids.reshape(1, 1, -1)
    for index in range(2):
        normed = layer_norm(stream, ln_gain[index])
        stream = layer(index, stream, normed, tag_row, w_qkv[index], w_out[index])
    return stream


def solution(mesh):
    in_specs = (
        P(("curve", "head"), None),
        P(("curve", "head"), None),
        P(("curve", "head")),
        P(),
        P(None, None, "head"),
        P(None, "head", None),
    )
    out_specs = P(("curve", "head"), None)
    return jax.shard_map(
        on_device, mesh=mesh, in_specs=in_specs, out_specs=out_specs, check_vma=False
    )
```

time: 296 us -> 152 us (0.51)
  Pallas kernels: 0 us -> 136 us
  matrix products: 121 us -> 0 us
  waiting for transfers between devices: 109 us -> 0 us
  starting transfers between devices: 16.9 us -> 0 us
  between operations: 13.3 us -> 0.09 us
  local copies, waits for them, and re-layouts: 15.9 us -> 8.11 us
  blocking collectives: 6.2 us -> 0 us
  loops' own time: 5.57 us -> 0 us
    pallas_call x0 -> x2, Pallas kernels: none -> 136 us  [layer(): pl.pallas_call(functools.partial(layer_kernel, peers, ranges, halo), out_...]
    dot_general x12 -> x0, matrix products: 65.1 us -> none  [the longest x8 45.9 us: one_block(): jnp.einsum('hqk,khd->qhd', probs, value_block, preferred_element_type=jnp...]
    all_gather x4 -> x0, waiting for transfers between devices: 59.7 us -> none  [the longest x2 59.7 us: on_device(): lax.all_gather(normed, 'head', axis=0, tiled=True)]
    sub x8 -> x0, matrix products: 56.2 us -> none  [one_block(): expo = jnp.exp(scores - row_max)]
    all_to_all x2 -> x0, waiting for transfers between devices: 28.5 us -> none  [on_device(): lax.all_to_all(attended, 'head', split_axis=0, concat_axis=1, tiled=True)]
    ppermute x4 -> x0, waiting for transfers between devices: 20.4 us -> none  [the longest x2 18.2 us: extended(): before = lax.ppermute(last, axis, up)]
    ppermute x4 -> x0, starting transfers between devices: 9.55 us -> none  [the longest x2 6.52 us: extended(): after = lax.ppermute(first, axis, down)]
    all_to_all x2 -> x0, starting transfers between devices: 7.03 us -> none  [on_device(): lax.all_to_all(attended, 'head', split_axis=0, concat_axis=1, tiled=True)]
  transfers between devices with their start and end apart: 10 -> 0, of which waited for: 6 -> 0; matrix products, arithmetic and copies ran while one was open for 44% -> 0% of each run, Pallas kernels for 0% -> 0%
where the time goes in v2:
time: 152 us; the launch traced here: 151 us
  Pallas kernels  136 us (89%)
  local copies, waits for them, and re-layouts  8.11 us (5%)
  other arithmetic  7.3 us (5%)
    pallas_call x2, Pallas kernels, layer(): pl.pallas_call(functools.partial(layer_kernel, peers, ranges, halo), out_...  136 us

profile of v2, /device:TPU:0, one launch (start us, length us, event | category | flops | bytes accessed | tf_op | source)
XLA Modules:
  0.0 151.4 jit_solution(12509614390691637078)
XLA Ops:
  0.0 0.0 copy-start
  0.0 0.8 compare_select_fusion
  0.8 0.8 fusion.5
  1.6 0.0 copy-done
  1.6 2.1 %gather_fusion = bf16[512,1024]{1,0:T(8,128)(2,1)S(1)} fusion(bf16[512,1024]{1,0:T(8,128)(2,1)S(1)} %copy-done, s32[1024]{0:T(1024)S(1)} %pad_clamp_fusion), kind=kCustom, calls=%fused_computation | custom fusion | bytes 2099200 | tf_op jit(solution)/shard_map/gather | solution.py:334
  3.6 0.0 copy-start.1
  3.7 0.0 copy-start.4
  3.7 0.2 convert_reduce_fusion.1
  3.9 0.4 multiply_reduce_fusion
  4.3 0.0 copy-start.3
  4.4 1.4 multiply_convert_fusion.x_ref
  5.7 0.0 copy-done.1
  5.7 0.0 copy-done.4
  5.7 1.1 slice_bitcast_fusion.2
  6.8 0.0 copy-done.3
  6.8 1.9 %slice_bitcast_fusion = (bf16[1024,768]{1,0:T(8,128)(2,1)}, bf16[1024,768]{1,0:T(8,128)(2,1)}) fusion(bf16[2,1024,768]{2,1,0:T(8,128)(2,1)S(1)} %copy-done.3), kind=kLoop, calls=%fused_computation.10 | loop fusion | bytes 6291456 | tf_op jit(solution)/shard_map/squeeze | solution.py:338
  8.7 64.9 %shard_map.64.stream_ref = bf16[512,1024]{1,0:T(8,128)(2,1)} custom-call(bf16[2,256,1024]{2,1,0:T(8,128)(2,1)} %multiply_convert_fusion.x_ref, s32[1,1,512]{2,1,0:T(1,128)} %bitcast.22, bf16[1024,768]{1,0:T(8,128)(2,1)} %get-tuple-element.6.w_ref, bf16[256,1024]{1,0:T(8,128)(2,1)} %get-tuple-element.8.wo_ref, bf16[512,1024]{1,0:T(8,128)(2,1)} %copy-done.1), custom_call_target="tpu_custom_call" | custom-call | flops 10737418240 | bytes 10485760 | tf_op jit(solution)/shard_map/pallas_call | solution.py:296
  73.6 0.0 copy-start.2
  73.6 1.5 %convert_reduce_fusion = f32[512]{0:T(512)S(1)} fusion(bf16[512,1024]{1,0:T(8,128)(2,1)} %shard_map.64.stream_ref), kind=kLoop, calls=%fused_computation.2 | loop fusion | flops 1048064 | bytes 1050624 | tf_op jit(solution)/shard_map/reduce_sum | solution.py:19
  75.1 1.6 %fusion.2 = f32[512]{0:T(512)S(1)} fusion(bf16[512,1024]{1,0:T(8,128)(2,1)} %shard_map.64.stream_ref, f32[512]{0:T(512)S(1)} %broadcast_multiply_fusion), kind=kLoop, calls=%fused_computation.5 | loop fusion | flops 2096640 | bytes 1052672 | tf_op jit(solution)/shard_map/reduce_sum | solution.py:20
  76.8 0.0 copy-done.2
  76.8 1.4 fusion.4
  78.1 71.0 %shard_map.65 = bf16[512,1024]{1,0:T(8,128)(2,1)} custom-call(bf16[2,256,1024]{2,1,0:T(8,128)(2,1)} %bitcast.18, s32[1,1,512]{2,1,0:T(1,128)} %bitcast.23, bf16[1024,768]{1,0:T(8,128)(2,1)} %get-tuple-element.5.w_ref, bf16[256,1024]{1,0:T(8,128)(2,1)} %get-tuple-element.7.wo_ref, bf16[512,1024]{1,0:T(8,128)(2,1)} %shard_map.64.stream_ref), custom_call_target="tpu_custom_call" | custom-call | flops 10737418240 | bytes 10485760 | tf_op jit(solution)/shard_map/pallas_call | solution.py:296
  149.2 2.3 %copy.8 = bf16[512,1024]{1,0:T(8,128)(2,1)} copy(bf16[512,1024]{1,0:T(8,128)(2,1)} %shard_map.65) | data formatting | bytes 2097152
  (7 shorter events, 0.1 us)
Async XLA Ops:
  0.0 1.6 %copy-start = (bf16[512,1024]{1,0:T(8,128)(2,1)S(1)}, bf16[512,1024]{1,0:T(8,128)(2,1)}, u32[]{:S(2)}) copy-start(bf16[512,1024]{1,0:T(8,128)(2,1)} %param.6) | copy-start | bytes 3145732
  3.6 2.1 %copy-start.1 = (bf16[512,1024]{1,0:T(8,128)(2,1)}, bf16[512,1024]{1,0:T(8,128)(2,1)S(1)}, u32[]{:S(2)}) copy-start(bf16[512,1024]{1,0:T(8,128)(2,1)S(1)} %gather_fusion) | copy-start | bytes 3145732
  3.7 2.0 %copy-start.4 = (bf16[2,256,1024]{2,1,0:T(8,128)(2,1)S(1)}, bf16[2,256,1024]{2,1,0:T(8,128)(2,1)}, u32[]{:S(2)}) copy-start(bf16[2,256,1024]{2,1,0:T(8,128)(2,1)} %param.11) | copy-start | bytes 3145732
  4.3 2.5 %copy-start.3 = (bf16[2,1024,768]{2,1,0:T(8,128)(2,1)S(1)}, bf16[2,1024,768]{2,1,0:T(8,128)(2,1)}, u32[]{:S(2)}) copy-start(bf16[2,1024,768]{2,1,0:T(8,128)(2,1)} %param.10) | copy-start | bytes 9437188
  73.6 3.2 %copy-start.2 = (bf16[512,1024]{1,0:T(8,128)(2,1)S(1)}, bf16[512,1024]{1,0:T(8,128)(2,1)}, u32[]{:S(2)}) copy-start(bf16[512,1024]{1,0:T(8,128)(2,1)} %shard_map.64.stream_ref) | copy-start | bytes 3145732
